TPU v7x, 32 devices: a whole 2x2x4 slice. The times are simulated.
32 devices in a mesh: kpt: 2 (over y), row: 4 (over x, core), col: 4 (over z).
Axes of the slice: x: 2, y: 2, z: 4, core: 2. Of those that a mesh axis runs over, the one named last changes fastest.
Arguments:
- left_blocks: bfloat16 [8, 64, 2, 2, 128, 128], P(('kpt', 'row'), 'col'), parts along dimension 0, may hold values from -0.5 to 0.5
- left_rows: int32 [8, 64, 2], P(('kpt', 'row'), 'col'), parts along dimension 0, may hold values from 0 to 7, as said below
- left_count: int32 [8, 64], P(('kpt', 'row'), 'col'), parts along dimension 0, may hold values from 1 to 2, as said below
- left_level: int32 [8, 64, 2], P(('kpt', 'row'), 'col'), parts along dimension 0, may hold values from 0 to 7
- right_blocks: bfloat16 [2, 64, 4, 4, 2, 128, 128], P('kpt', 'row', 'col'), parts along dimension 0, may hold values from -6 to 6
- right_cols: int32 [2, 64, 4, 4], P('kpt', 'row', 'col'), parts along dimension 0, may hold values from 0 to 15, as said below
- right_count: int32 [2, 64, 4], P('kpt', 'row', 'col'), parts along dimension 0, may hold values from 1 to 4, as said below
- right_level: int32 [2, 64, 4, 4], P('kpt', 'row', 'col'), parts along dimension 0, may hold values from 0 to 7
Outputs:
- product_blocks: bfloat16 [64, 64, 2, 128, 128], P(('kpt', 'row'), 'col'), parts along dimension 0
There are 2 independent parts, one for each index of `kpt`. A program takes and returns all parts, laid end to end along the dimension named above; each array names one. Nothing has to cross between parts.
Inputs may be any that keep to these rules, and one draw needn't show every extreme that they name: `left_rows`: the 2 slots of one row group and block column name distinct block rows. `left_count`: in every row group some block column has all 2 slots live. `right_cols`: the 4 slots of one block row and column group name distinct block columns. `right_count`: in every column group some block row has all 4 slots live.
All inputs are finite; a program needn't handle non-finite values.
Results may differ from a plain program's by a relative error of at most 0.001.
Values may be sent and summed in bfloat16 or wider, within the bound.
A program may use at most 256 MiB of HBM per device.

v0:
```python
import functools

import jax
import jax.numpy as jnp
from jax import lax
from jax.experimental import pallas as pl
from jax.experimental.pallas import tpu as pltpu
from jax.sharding import PartitionSpec as P

GR = 8
LEVEL_CUT = 7
DEAD = -1000
UNROLL = 16
LEFT_CUTS = 2
VMEM_BYTES = 62 * 1024 * 1024
RIGHT_CUTS = 4
MESH = pl.DeviceIdType.MESH


def gather_kernel(
    n_row, n_col, left, right, meta,
    left_all, right_all, left_meta_all, right_meta_all,
    up_send, up_recv, down_send, down_recv,
    x_send, x_recv, own_send, own_recv, pass_send, pass_recv,
    lm_send, lm_recv, rm_send, rm_recv, left_sem, right_sem,
):
    row = lax.axis_index("row")
    col = lax.axis_index("col")
    n_chip = n_row // 2
    chip, core = row // 2, row % 2
    partner = chip * 2 + 1 - core

    barrier = pltpu.get_barrier_semaphore()
    for step in range(1, n_row):
        pl.semaphore_signal(
            barrier, inc=1, device_id={"row": (row + step) % n_row}, device_id_type=MESH
        )
    for step in range(1, n_col):
        pl.semaphore_signal(
            barrier, inc=1, device_id={"col": (col + step) % n_col}, device_id_type=MESH
        )
    pl.semaphore_wait(barrier, n_row + n_col - 2)

    left_size = left.shape[0] // LEFT_CUTS
    right_size = right.shape[1] // RIGHT_CUTS

    def left_copy(step, cut, up):
        panel = col - step if up else col + step
        span = pl.ds(cut * left_size, left_size)
        source = left.at[span] if step == 0 else left_all.at[panel, span]
        send, recv = (up_send, up_recv) if up else (down_send, down_recv)
        return pltpu.make_async_remote_copy(
            src_ref=source, dst_ref=left_all.at[panel, span],
            send_sem=send.at[step, cut], recv_sem=recv.at[step, cut],
            device_id={"col": col + 1 if up else col - 1}, device_id_type=MESH,
        )

    def left_sends(step, up):
        if up:
            return (col + 1 < n_col) & (col - step >= 0)
        return (col - 1 >= 0) & (col + step < n_col)

    def left_receives(step, up):
        return col - 1 - step >= 0 if up else col + 1 + step < n_col

    def across(step, cut):
        span = pl.ds(cut * right_size, right_size)
        other = ((chip + step) % n_chip) * 2 + core
        return pltpu.make_async_remote_copy(
            src_ref=right.at[:, span], dst_ref=right_all.at[:, row, span],
            send_sem=x_send.at[step - 1, cut], recv_sem=x_recv.at[step - 1, cut],
            device_id={"row": other}, device_id_type=MESH,
        )

    def passed(step, cut):
        span = pl.ds(cut * right_size, right_size)
        panel = ((chip + n_chip - step) % n_chip) * 2 + core
        return pltpu.make_async_remote_copy(
            src_ref=right_all.at[:, panel, span], dst_ref=right_all.at[:, panel, span],
            send_sem=pass_send.at[step - 1, cut], recv_sem=pass_recv.at[step - 1, cut],
            device_id={"row": partner}, device_id_type=MESH,
        )

    own = pltpu.make_async_remote_copy(
        src_ref=right, dst_ref=right_all.at[:, row],
        send_sem=own_send, recv_sem=own_recv,
        device_id={"row": partner}, device_id_type=MESH,
    )

    def meta_copies():
        for step in range(1, n_col):
            yield pltpu.make_async_remote_copy(
                src_ref=meta, dst_ref=left_meta_all.at[col],
                send_sem=lm_send.at[step - 1], recv_sem=lm_recv.at[step - 1],
                device_id={"col": (col + step) % n_col}, device_id_type=MESH,
            )
        for step in range(1, n_row):
            yield pltpu.make_async_remote_copy(
                src_ref=meta, dst_ref=right_meta_all.at[row],
                send_sem=rm_send.at[step - 1], recv_sem=rm_recv.at[step - 1],
                device_id={"row": (row + step) % n_row}, device_id_type=MESH,
            )

    for copy in meta_copies():
        copy.start()
    for cut in range(LEFT_CUTS):
        for up in (True, False):
            pl.when(left_sends(0, up))(left_copy(0, cut, up).start)
    for step in range(1, n_chip):
        for cut in range(RIGHT_CUTS):
            across(step, cut).start()
    own.start()
    kept = (
        pltpu.make_async_copy(left, left_all.at[col], left_sem),
        pltpu.make_async_copy(right, right_all.at[:, row], right_sem),
    )
    for copy in kept:
        copy.start()
    left_meta_all[col] = meta[...]
    right_meta_all[row] = meta[...]

    def take_left(step, cut):
        for up in (True, False):
            pl.when(left_receives(step, up))(left_copy(step, cut, up).wait_recv)
            if step + 1 < n_col - 1:
                pl.when(left_sends(step + 1, up))(left_copy(step + 1, cut, up).start)

    def take_right(step, cut):
        across(step, cut).wait_recv()
        passed(step, cut).start()

    left_jobs = [
        ((step * LEFT_CUTS + cut + 1) / LEFT_CUTS, functools.partial(take_left, step, cut))
        for step in range(n_col - 1) for cut in range(LEFT_CUTS)
    ]
    right_jobs = [
        (2 * ((step - 1) * RIGHT_CUTS + cut + 1) / RIGHT_CUTS + 0.1,
         functools.partial(take_right, step, cut))
        for step in range(1, n_chip) for cut in range(RIGHT_CUTS)
    ]
    for _, job in sorted(left_jobs + right_jobs, key=lambda entry: entry[0]):
        job()

    own.wait()
    for copy in kept:
        copy.wait()
    for step in range(1, n_chip):
        for cut in range(RIGHT_CUTS):
            across(step, cut).wait_send()
            passed(step, cut).wait()
    for step in range(n_col - 1):
        for cut in range(LEFT_CUTS):
            for up in (True, False):
                pl.when(left_sends(step, up))(left_copy(step, cut, up).wait_send)
    for copy in meta_copies():
        copy.wait()


def product_kernel(
    sizes, left, right, left_meta, right_meta, out, total, stage, pairs, touched, out_sem,
):
    n_row, n_col, sets, per, ma, mb, kb_cols = sizes
    blocks = GR * kb_cols
    tall = sets * per

    @pl.loop(0, blocks + 1)
    def _(block):
        touched[block] = 0

    count = jnp.int32(0)
    for panel in range(n_col):
        which, at = panel // n_row, panel % n_row

        def gather(k, count):
            line = which * per + k
            live = right_meta[at, tall + 1 + which, k]
            rights = []
            for n in range(mb):
                level = right_meta[at, line, 2 * ma + mb + n]
                rights.append(
                    (right_meta[at, line, 2 * ma + n], jnp.where(n < live, level, DEAD))
                )
            live = left_meta[panel, tall, k]
            slot = panel * per + k
            for m in range(ma):
                target = left_meta[panel, k, m] * kb_cols
                level = jnp.where(m < live, left_meta[panel, k, ma + m], DEAD)
                for n in range(mb):
                    code = (slot * ma + m) * 1024 + slot * mb + n
                    pairs[count] = code * 1024 + target + rights[n][0]
                    count = count + jnp.where(level + rights[n][1] >= LEVEL_CUT, 1, 0)
            return count

        count = lax.fori_loop(0, per, gather, count, unroll=4)
    for extra in range(UNROLL):
        pairs[count + extra] = blocks

    @pl.loop(0, (count + UNROLL - 1) // UNROLL)
    def _(group):
        done = []
        for lane in range(UNROLL):
            code = pairs[group * UNROLL + lane]
            target = code & 1023
            block = left[code >> 20]
            width = block.shape[1]
            real, imag = block[:width], block[width:]
            matrix = jnp.concatenate(
                [jnp.concatenate([real, -imag], axis=1), jnp.concatenate([imag, real], axis=1)],
                axis=0,
            )
            other = right[(code >> 10) & 1023]
            done.append((target, jnp.dot(matrix, other, preferred_element_type=jnp.float32)))
        for target, product in done:
            old = touched[target] > 0
            total[target] = jnp.where(old, total[target], 0.0) + product
            touched[target] = 1

    def out_copy(line):
        span = pl.ds(line * kb_cols, kb_cols)
        return pltpu.make_async_copy(stage.at[span], out.at[span], out_sem.at[line])

    @pl.loop(0, GR)
    def _(line):
        @pl.loop(0, kb_cols, unroll=4)
        def _(k):
            block = line * kb_cols + k
            stage[block] = jnp.where(touched[block] > 0, total[block], 0.0).astype(stage.dtype)

        out_copy(line).start()

    @pl.loop(0, GR)
    def _(line):
        out_copy(line).wait()


def place(array, top, lane, rows):
    tall, wide = array.shape
    return jnp.pad(array, ((top, rows - tall - top), (lane, 128 - lane - wide)))


def body(
    n_row, n_col, left_blocks, left_rows, left_count, left_level,
    right_blocks, right_cols, right_count, right_level,
):
    _, per, ma, _, width, _ = left_blocks.shape
    sets, right_per, _, mb = right_blocks.shape[:4]
    assert right_per == per and sets * n_row == n_col and n_row % 2 == 0
    left = left_blocks.reshape(per * ma, 2 * width, width)
    right = right_blocks.reshape(sets, per * mb, 2 * width, width)
    tall = sets * per
    rows = -(-(tall + 1 + sets) // 8) * 8
    meta = (
        place(jnp.concatenate([left_rows[0], left_level[0]], axis=1), 0, 0, rows)
        + place(left_count, tall, 0, rows)
        + place(
            jnp.concatenate([right_cols, right_level], axis=3).reshape(tall, 2 * mb),
            0, 2 * ma, rows,
        )
        + place(right_count.reshape(sets, per), tall + 1, 0, rows)
    )
    any_space = pl.BlockSpec(memory_space=pl.ANY)
    vmem = pl.BlockSpec(memory_space=pltpu.VMEM)
    smem = pl.BlockSpec(memory_space=pltpu.SMEM)
    dma = pltpu.SemaphoreType.DMA
    n_chip = n_row // 2
    left_shape = (n_col,) + left.shape
    right_shape = (sets, n_row) + right.shape[1:]
    limit = VMEM_BYTES - (n_col * left.size + n_row * right.size) * left.dtype.itemsize
    gathered = pl.pallas_call(
        functools.partial(gather_kernel, n_row, n_col),
        out_shape=(
            pltpu.VMEM(left_shape, left.dtype),
            pltpu.VMEM(right_shape, right.dtype),
            jax.ShapeDtypeStruct((n_col,) + meta.shape, jnp.int32),
            jax.ShapeDtypeStruct((n_row,) + meta.shape, jnp.int32),
        ),
        in_specs=[any_space, any_space, vmem],
        out_specs=(vmem, vmem, vmem, vmem),
        scratch_shapes=[
            *[dma((n_col - 1, LEFT_CUTS))] * 4,
            *[dma((n_chip - 1, RIGHT_CUTS))] * 2,
            *[dma] * 2,
            *[dma((n_chip - 1, RIGHT_CUTS))] * 2,
            *[dma((n_col - 1,))] * 2,
            *[dma((n_row - 1,))] * 2,
            *[dma] * 2,
        ],
        compiler_params=pltpu.CompilerParams(
            collective_id=0, has_side_effects=True, vmem_limit_bytes=limit
        ),
        name="gather_panels",
    )(left, right, meta)
    left_all, right_all, left_meta_all, right_meta_all = gathered
    kb_cols = n_row * sets * per // n_col
    blocks = GR * kb_cols
    out = pl.pallas_call(
        functools.partial(product_kernel, (n_row, n_col, sets, per, ma, mb, kb_cols)),
        out_shape=jax.ShapeDtypeStruct((blocks, 2 * width, width), jnp.bfloat16),
        in_specs=[vmem] * 2 + [smem] * 2,
        out_specs=any_space,
        scratch_shapes=[
            pltpu.VMEM((blocks + 1, 2 * width, width), jnp.float32),
            pltpu.VMEM((blocks, 2 * width, width), jnp.bfloat16),
            pltpu.SMEM((n_col * per * ma * mb + UNROLL,), jnp.int32),
            pltpu.SMEM((blocks + 1,), jnp.int32),
            dma((GR,)),
        ],
        compiler_params=pltpu.CompilerParams(vmem_limit_bytes=limit),
        name="pair_products",
    )(
        pltpu.with_memory_space_constraint(
            left_all.reshape((-1,) + left.shape[1:]), pltpu.VMEM
        ),
        pltpu.with_memory_space_constraint(
            right_all.reshape((-1,) + right.shape[2:]), pltpu.VMEM
        ),
        left_meta_all, right_meta_all,
    )
    return out.reshape(GR, kb_cols, 2, width, width)


def solution(mesh):
    in_specs = (
        P(("kpt", "row"), "col", None, None, None, None),
        P(("kpt", "row"), "col", None),
        P(("kpt", "row"), "col"),
        P(("kpt", "row"), "col", None),
        P("kpt", "row", "col", None, None, None, None),
        P("kpt", "row", "col", None),
        P("kpt", "row", "col"),
        P("kpt", "row", "col", None),
    )
    out_specs = P(("kpt", "row"), "col", None, None, None)
    return jax.shard_map(
        functools.partial(body, mesh.shape["row"], mesh.shape["col"]),
        mesh=mesh, in_specs=in_specs, out_specs=out_specs, check_vma=False,
    )
```

profile of v0, /device:TPU:0, one launch (start us, length us, event | category | flops | bytes accessed | tf_op | source)
XLA Modules:
  0.0 163.7 jit_solution(12855315076120624910)
XLA Ops:
  0.0 0.7 pad_add_fusion.1
  0.7 0.7 add_bitcast_fusion
  1.4 0.1 copy.13
  1.5 0.1 copy.12
  1.6 1.3 pad_add_fusion.meta
  2.9 143.7 %gather_panels.1 = (bf16[4,32,256,128]{3,2,1,0:T(8,128)(2,1)S(1)}, bf16[1,4,64,256,128]{4,3,2,1,0:T(8,128)(2,1)S(1)}, s32[4,24,128]{2,1,0:T(8,128)}, s32[4,24,128]{2,1,0:T(8,128)}) custom-call(bf16[32,256,128]{2,1,0:T(8,128)(2,1)} %bitcast.13, bf16[1,64,256,128]{3,2,1,0:T(8,128)(2,1)} %bitcast.12, s32[24,128]{1,0:T(8,128)} %pad_add_fusion.meta), custom_call_target="tpu_custom_call" | custom-call | tf_op jit(solution)/shard_map/gather_panels/pallas_call | solution.py:269
  146.6 17.1 %pair_products.1 = bf16[128,256,128]{2,1,0:T(8,128)(2,1)} custom-call(bf16[128,256,128]{2,1,0:T(8,128)(2,1)S(1)} %bitcast.11, bf16[256,256,128]{2,1,0:T(8,128)(2,1)S(1)} %bitcast.10, s32[4,24,128]{2,1,0:T(8,128)} %get-tuple-element.11.left_meta, s32[4,24,128]{2,1,0:T(8,128)} %get-tuple-element.12.right_meta), custom_call_target="tpu_custom_call" | custom-call | tf_op jit(solution)/shard_map/pair_products/pallas_call | solution.py:296
where the time goes:
time: 163 us; the launch traced here: 164 us
  Pallas kernels  161 us (99%)
  other arithmetic  2.75 us (2%)
    pallas_call x1, Pallas kernels, body(): pl.pallas_call(functools.partial(gather_kernel, n_row, n_col), out_shape=...  144 us
    pallas_call x1, Pallas kernels, body(): pl.pallas_call(functools.partial(product_kernel, (n_row, n_col, sets, per...  17.1 us

commit v1 on v0

v1 whole, which is shorter than its diff:
```python
import functools

import jax
import jax.numpy as jnp
from jax import lax
from jax.experimental import pallas as pl
from jax.experimental.pallas import tpu as pltpu
from jax.sharding import PartitionSpec as P

GR = 8
LEVEL_CUT = 7
DEAD = -1000
GROUP = 4
MAIN_CUTS = 2
RIGHT_CUTS = 8
VMEM_BYTES = 62 * 1024 * 1024
MESH = pl.DeviceIdType.MESH
ROW_LEFT, ROW_MAX, ROW_TARGET, ROW_COLS, ROW_RIGHT = 0, 1, 3, 4, 5


def variants(slots):
    main = slots * 22 // 32
    found = []
    for size in range(main, slots, max(1, slots // 16)):
        found.append((size, 0, slots))
    found.append((slots, 0, slots))
    return found


def plan_kernel(
    sizes, options, tile, left_meta, right_meta, table, choice, tiles, send, recv,
):
    n_kpt, n_row, n_col, sets, per, ma, mb = sizes
    slots = per * ma
    kpt, row, col = (lax.axis_index(name) for name in ("kpt", "row", "col"))
    total = n_kpt * n_row * n_col
    me = (kpt * n_row + row) * n_col + col

    def place_of(step):
        other = (me + step) % total
        return {
            "kpt": other // (n_row * n_col), "row": (other // n_col) % n_row, "col": other % n_col
        }

    def copy_of(step):
        return pltpu.make_async_remote_copy(
            src_ref=tile, dst_ref=tiles.at[me], send_sem=send.at[step], recv_sem=recv.at[step],
            device_id=place_of(step), device_id_type=MESH,
        )

    barrier = pltpu.get_barrier_semaphore()

    @pl.loop(1, total)
    def _(step):
        pl.semaphore_signal(barrier, inc=1, device_id=place_of(step), device_id_type=MESH)

    tiles[me] = tile[...]
    pl.semaphore_wait(barrier, total - 1)

    @pl.loop(1, total)
    def _(step):
        copy_of(step).start()

    @pl.loop(1, total)
    def _(step):
        copy_of(step).wait_recv()

    def at_device(k, r, c):
        return (k * n_row + r) * n_col + c

    for c in range(n_col):
        left_meta[c] = tiles[at_device(kpt, row, c)]
    for r in range(n_row):
        right_meta[r] = tiles[at_device(kpt, r, col)]

    def right_max(k, panel, q):
        return tiles[at_device(k, panel % n_row, q), pl.ds(ROW_MAX + panel // n_row, 1), :]

    def count_needed(levels, most):
        return jnp.sum(
            jnp.where(levels + most >= LEVEL_CUT, 1.0, 0.0), axis=1, keepdims=True
        )

    main = options[0][0]

    def measure_part(k, carry):
        most_end, most_mid = carry
        for panel in range(n_col):
            levels = jnp.concatenate(
                [tiles[at_device(k, r, panel), pl.ds(ROW_LEFT, 1), :] for r in range(n_row)],
                axis=0,
            )
            rights = [right_max(k, panel, q) for q in range(n_col)]
            if panel > 0:
                most_end = jnp.maximum(most_end, count_needed(levels, rights[0]))
            if panel < n_col - 1:
                most_end = jnp.maximum(most_end, count_needed(levels, rights[-1]))
            if panel > 1:
                most_mid = jnp.maximum(
                    most_mid, count_needed(levels, functools.reduce(jnp.maximum, rights[:panel]))
                )
            if panel < n_col - 2:
                most_mid = jnp.maximum(
                    most_mid,
                    count_needed(levels, functools.reduce(jnp.maximum, rights[panel + 1:])),
                )
        return most_end, most_mid

    zero = jnp.zeros((n_row, 1), jnp.float32)
    most_end, most_mid = lax.fori_loop(0, n_kpt, measure_part, (zero, zero))
    index = jnp.zeros((n_row, 1), jnp.float32)
    for size, _, middle in options[:-1]:
        index = index + jnp.where((most_end > size) | (most_mid > middle), 1.0, 0.0)
    choice[0] = jnp.max(index).astype(jnp.int32)

    lane = lax.broadcasted_iota(jnp.int32, (128, 128), 1)
    line = lax.broadcasted_iota(jnp.int32, (128, 128), 0)
    lane_row = lane[:1].astype(jnp.float32)

    def ranks(panel, up):
        levels = tiles[at_device(kpt, row, panel), pl.ds(ROW_LEFT, 1), :]
        end = right_max(kpt, panel, n_col - 1 if up else 0)
        union = jnp.full((1, 128), DEAD, jnp.int32)
        for q in range(n_col):
            beyond = q > panel if up else q < panel
            union = jnp.maximum(union, jnp.where(beyond, right_max(kpt, panel, q), DEAD))
        kind = jnp.where(
            levels + end >= LEVEL_CUT, 0.0, jnp.where(levels + union >= LEVEL_CUT, 1.0, 2.0)
        )
        key = jnp.where(lane_row < slots, kind, 3.0) * 128.0 + lane_row
        key_row = jnp.broadcast_to(key, (128, 128))
        key_line = jnp.sum(jnp.where(lane == line, key_row, 0.0), axis=1, keepdims=True)
        before = jnp.where(key_line < key_row, 1.0, 0.0)
        rank_row = jnp.sum(before, axis=0, keepdims=True)
        after = jnp.where(key_row < key_line, 1.0, 0.0)
        rank_line = jnp.sum(after, axis=1, keepdims=True)
        return rank_row, rank_line

    def write(at, values):
        table[pl.ds(at, 1), :] = values.astype(jnp.int32)

    for panel in range(n_col):
        rank_down = ranks(panel, False)[0] if panel > 0 else lane_row
        rank_up = ranks(panel, True)[0] if panel < n_col - 1 else lane_row
        place = jnp.where(panel > col, rank_down, jnp.where(panel < col, rank_up, lane_row))
        write(panel, place + panel * slots)
    for at, up in ((n_col, False), (n_col + 1, True)):
        rank_line = ranks(col, up)[1]
        hit = jnp.where(rank_line == lane.astype(jnp.float32), line.astype(jnp.float32), 0.0)
        write(at, jnp.sum(hit, axis=0, keepdims=True))

    @pl.loop(1, total)
    def _(step):
        copy_of(step).wait_send()


def gather_kernel(
    n_row, n_col, option, left, right, table,
    left_all, right_all,
    own_left, packed_down, packed_up,
    up_send, up_recv, down_send, down_recv,
    x_send, x_recv, own_send, own_recv, pass_send, pass_recv,
    stage_sem, left_sem, right_sem,
):
    row = lax.axis_index("row")
    col = lax.axis_index("col")
    n_chip = n_row // 2
    chip, core = row // 2, row % 2
    partner = chip * 2 + 1 - core
    slots = left.shape[0]
    main, _, middle = option

    staged = pltpu.make_async_copy(left, own_left, stage_sem)
    staged.start()
    barrier = pltpu.get_barrier_semaphore()
    for step in range(1, n_row):
        pl.semaphore_signal(
            barrier, inc=1, device_id={"row": (row + step) % n_row}, device_id_type=MESH
        )
    for step in (1, n_col - 1):
        pl.semaphore_signal(
            barrier, inc=1, device_id={"col": (col + step) % n_col}, device_id_type=MESH
        )

    bounds = [main * at // MAIN_CUTS for at in range(MAIN_CUTS + 1)]
    cuts = [(low, high, False) for low, high in zip(bounds, bounds[1:])]
    if middle > main:
        cuts.append((main, middle, True))
    right_size = right.shape[1] // RIGHT_CUTS

    def left_copy(step, cut, up):
        low, high, _ = cuts[cut]
        panel = col - step if up else col + step
        source = (
            (packed_up if up else packed_down).at[pl.ds(low, high - low)]
            if step == 0 else left_all.at[panel, pl.ds(low, high - low)]
        )
        send, recv = (up_send, up_recv) if up else (down_send, down_recv)
        return pltpu.make_async_remote_copy(
            src_ref=source, dst_ref=left_all.at[panel, pl.ds(low, high - low)],
            send_sem=send.at[step, cut], recv_sem=recv.at[step, cut],
            device_id={"col": col + 1 if up else col - 1}, device_id_type=MESH,
        )

    def left_sends(step, cut, up):
        mid = cuts[cut][2]
        if up:
            return (col + 1 < n_col - (1 if mid else 0)) & (col - step >= 0)
        return (col - 1 >= (1 if mid else 0)) & (col + step < n_col)

    def left_receives(step, cut, up):
        mid = cuts[cut][2]
        if up:
            return (col - 1 - step >= 0) & (col < n_col - (1 if mid else 0))
        return (col + 1 + step < n_col) & (col >= (1 if mid else 0))

    def across(step, cut):
        span = pl.ds(cut * right_size, right_size)
        other = ((chip + step) % n_chip) * 2 + core
        return pltpu.make_async_remote_copy(
            src_ref=right.at[:, span], dst_ref=right_all.at[:, row, span],
            send_sem=x_send.at[step - 1, cut], recv_sem=x_recv.at[step - 1, cut],
            device_id={"row": other}, device_id_type=MESH,
        )

    def passed(step, cut):
        span = pl.ds(cut * right_size, right_size)
        panel = ((chip + n_chip - step) % n_chip) * 2 + core
        return pltpu.make_async_remote_copy(
            src_ref=right_all.at[:, panel, span], dst_ref=right_all.at[:, panel, span],
            send_sem=pass_send.at[step - 1, cut], recv_sem=pass_recv.at[step - 1, cut],
            device_id={"row": partner}, device_id_type=MESH,
        )

    own = pltpu.make_async_remote_copy(
        src_ref=right, dst_ref=right_all.at[:, row],
        send_sem=own_send, recv_sem=own_recv,
        device_id={"row": partner}, device_id_type=MESH,
    )
    kept = (
        pltpu.make_async_copy(left, left_all.at[col], left_sem),
        pltpu.make_async_copy(right, right_all.at[:, row], right_sem),
    )

    staged.wait()

    @pl.loop(0, middle)
    def _(at):
        packed_down[at] = own_left[table[n_col, at]]
        packed_up[at] = own_left[table[n_col + 1, at]]

    pl.semaphore_wait(barrier, n_row + 1)
    for cut in range(len(cuts)):
        for up in (True, False):
            pl.when(left_sends(0, cut, up))(left_copy(0, cut, up).start)
    for step in range(1, n_chip):
        for cut in range(RIGHT_CUTS):
            across(step, cut).start()
    own.start()
    for copy in kept:
        copy.start()

    def take_left(step, cut):
        for up in (True, False):
            pl.when(left_receives(step, cut, up))(left_copy(step, cut, up).wait_recv)
            if step + 1 < n_col - 1:
                pl.when(left_sends(step + 1, cut, up))(left_copy(step + 1, cut, up).start)

    def take_right(step, cut):
        across(step, cut).wait_recv()
        passed(step, cut).start()

    left_jobs = [
        (step * middle + cuts[cut][1], functools.partial(take_left, step, cut))
        for step in range(n_col - 1) for cut in range(len(cuts))
    ]
    right_jobs = [
        (((step - 1) * RIGHT_CUTS + cut + 1) * right.shape[0] * right_size + 0.5,
         functools.partial(take_right, step, cut))
        for step in range(1, n_chip) for cut in range(RIGHT_CUTS)
    ]
    for _, job in sorted(left_jobs + right_jobs, key=lambda entry: entry[0]):
        job()

    own.wait()
    for copy in kept:
        copy.wait()
    for step in range(1, n_chip):
        for cut in range(RIGHT_CUTS):
            across(step, cut).wait_send()
            passed(step, cut).wait()
    for step in range(n_col - 1):
        for cut in range(len(cuts)):
            for up in (True, False):
                pl.when(left_sends(step, cut, up))(left_copy(step, cut, up).wait_send)


def product_kernel(
    sizes, left, right, left_meta, right_meta, table, out, total, stage, pairs, touched, out_sem,
):
    n_row, n_col, sets, per, ma, mb, kb_cols = sizes
    blocks = GR * kb_cols

    @pl.loop(0, blocks + 1)
    def _(block):
        touched[block] = 0

    count = jnp.int32(0)
    for panel in range(n_col):
        which, at = panel // n_row, panel % n_row

        def gather(k, count):
            rights = []
            for n in range(mb):
                spot = (which * per + k) * mb + n
                rights.append((right_meta[at, ROW_COLS, spot], right_meta[at, ROW_RIGHT, spot]))
            slot = panel * per + k
            for m in range(ma):
                spot = k * ma + m
                target = left_meta[panel, ROW_TARGET, spot] * kb_cols
                level = left_meta[panel, ROW_LEFT, spot]
                code = table[panel, spot] * 1024 + slot * mb
                for n in range(mb):
                    pairs[count] = (code + n) * 1024 + target + rights[n][0]
                    count = count + jnp.where(level + rights[n][1] >= LEVEL_CUT, 1, 0)
            return count

        count = lax.fori_loop(0, per, gather, count, unroll=4)
    for extra in range(GROUP):
        pairs[count + extra] = blocks

    @pl.loop(0, (count + GROUP - 1) // GROUP)
    def _(group):
        done = []
        for lane in range(GROUP):
            code = pairs[group * GROUP + lane]
            target = code & 1023
            block = left[code >> 20]
            width = block.shape[1]
            wide = jnp.concatenate([block[:width], block[width:]], axis=1)
            other = right[(code >> 10) & 1023]
            real, imag = other[:width], other[width:]
            matrix = jnp.concatenate(
                [jnp.concatenate([real, imag], axis=1), jnp.concatenate([-imag, real], axis=1)],
                axis=0,
            )
            done.append((target, jnp.dot(wide, matrix, preferred_element_type=jnp.float32)))
        for target, product in done:
            old = touched[target] > 0
            total[target] = jnp.where(old, total[target], 0.0) + product
            touched[target] = 1

    def out_copy(line):
        span = pl.ds(line * kb_cols, kb_cols)
        return pltpu.make_async_copy(stage.at[span], out.at[span], out_sem.at[line])

    @pl.loop(0, GR)
    def _(line):
        @pl.loop(0, kb_cols, unroll=4)
        def _(k):
            block = line * kb_cols + k
            value = jnp.where(touched[block] > 0, total[block], 0.0).astype(stage.dtype)
            width = value.shape[0]
            stage[block, :width] = value[:, :width]
            stage[block, width:] = value[:, width:]

        out_copy(line).start()

    @pl.loop(0, GR)
    def _(line):
        out_copy(line).wait()


def body(
    n_kpt, n_row, n_col, left_blocks, left_rows, left_count, left_level,
    right_blocks, right_cols, right_count, right_level,
):
    _, per, ma, _, width, _ = left_blocks.shape
    sets, right_per, _, mb = right_blocks.shape[:4]
    assert right_per == per and sets * n_row == n_col and n_row % 2 == 0 and sets <= 2
    assert per * ma <= 128 and sets * per * mb <= 128
    slots = per * ma
    left = left_blocks.reshape(slots, 2 * width, width)
    right = right_blocks.reshape(sets, per * mb, 2 * width, width)

    def line(array):
        flat = array.reshape(1, -1)
        return jnp.pad(flat, ((0, 0), (0, 128 - flat.shape[1])), constant_values=DEAD)

    left_levels = jnp.where(
        jnp.arange(ma, dtype=jnp.int32) < left_count[..., None], left_level, DEAD
    )
    right_levels = jnp.where(
        jnp.arange(mb, dtype=jnp.int32) < right_count[..., None], right_level, DEAD
    ).reshape(sets, per, mb)
    most = jnp.repeat(jnp.max(right_levels, axis=2), ma, axis=1)
    lines = [line(left_levels)]
    lines += [line(most[at % sets]) for at in range(2)]
    lines += [line(left_rows), line(right_cols), line(right_levels)]
    tile = jnp.concatenate(lines + [lines[0]] * 2, axis=0)

    any_space = pl.BlockSpec(memory_space=pl.ANY)
    vmem = pl.BlockSpec(memory_space=pltpu.VMEM)
    smem = pl.BlockSpec(memory_space=pltpu.SMEM)
    dma = pltpu.SemaphoreType.DMA
    n_chip = n_row // 2
    total = n_kpt * n_row * n_col
    options = variants(slots)
    table_rows = -(-(n_col + 4) // 8) * 8
    left_meta, right_meta, table, choice = pl.pallas_call(
        functools.partial(plan_kernel, (n_kpt, n_row, n_col, sets, per, ma, mb), options),
        out_shape=(
            jax.ShapeDtypeStruct((n_col, 8, 128), jnp.int32),
            jax.ShapeDtypeStruct((n_row, 8, 128), jnp.int32),
            jax.ShapeDtypeStruct((table_rows, 128), jnp.int32),
            jax.ShapeDtypeStruct((1,), jnp.int32),
        ),
        in_specs=[vmem],
        out_specs=(vmem, vmem, vmem, smem),
        scratch_shapes=[pltpu.VMEM((total, 8, 128), jnp.int32), dma((total,)), dma((total,))],
        compiler_params=pltpu.CompilerParams(collective_id=0, has_side_effects=True),
        name="plan",
    )(tile)

    kb_cols = n_row * sets * per // n_col
    blocks = GR * kb_cols
    left_shape = (n_col,) + left.shape
    right_shape = (sets, n_row) + right.shape[1:]
    limit = VMEM_BYTES - (n_col * left.size + n_row * right.size) * left.dtype.itemsize

    def run(at, left, right, left_meta, right_meta, table):
        cuts = MAIN_CUTS + 1
        left_all, right_all = pl.pallas_call(
            functools.partial(gather_kernel, n_row, n_col, options[at]),
            out_shape=(
                pltpu.VMEM(left_shape, left.dtype),
                pltpu.VMEM(right_shape, right.dtype),
            ),
            in_specs=[any_space, any_space, smem],
            out_specs=(vmem, vmem),
            scratch_shapes=[
                *[pltpu.VMEM(left.shape, left.dtype)] * 3,
                *[dma((n_col - 1, cuts))] * 4,
                *[dma((n_chip - 1, RIGHT_CUTS))] * 2,
                *[dma] * 2,
                *[dma((n_chip - 1, RIGHT_CUTS))] * 2,
                *[dma] * 3,
            ],
            compiler_params=pltpu.CompilerParams(
                collective_id=1 + at, has_side_effects=True, vmem_limit_bytes=limit
            ),
            name=f"gather_panels_{at}",
        )(left, right, table)
        return pl.pallas_call(
            functools.partial(product_kernel, (n_row, n_col, sets, per, ma, mb, kb_cols)),
            out_shape=jax.ShapeDtypeStruct((blocks, 2 * width, width), jnp.bfloat16),
            in_specs=[vmem] * 2 + [smem] * 3,
            out_specs=any_space,
            scratch_shapes=[
                pltpu.VMEM((blocks + 1, width, 2 * width), jnp.float32),
                pltpu.VMEM((blocks, 2 * width, width), jnp.bfloat16),
                pltpu.SMEM((n_col * per * ma * mb + GROUP,), jnp.int32),
                pltpu.SMEM((blocks + 1,), jnp.int32),
                dma((GR,)),
            ],
            compiler_params=pltpu.CompilerParams(vmem_limit_bytes=limit),
            name="pair_products",
        )(
            pltpu.with_memory_space_constraint(
                left_all.reshape((-1,) + left.shape[1:]), pltpu.VMEM
            ),
            pltpu.with_memory_space_constraint(
                right_all.reshape((-1,) + right.shape[2:]), pltpu.VMEM
            ),
            left_meta, right_meta, table,
        )

    out = lax.switch(
        choice[0], [functools.partial(run, at) for at in range(len(options))],
        left, right, left_meta, right_meta, table,
    )
    return out.reshape(GR, kb_cols, 2, width, width)


def solution(mesh):
    in_specs = (
        P(("kpt", "row"), "col", None, None, None, None),
        P(("kpt", "row"), "col", None),
        P(("kpt", "row"), "col"),
        P(("kpt", "row"), "col", None),
        P("kpt", "row", "col", None, None, None, None),
        P("kpt", "row", "col", None),
        P("kpt", "row", "col"),
        P("kpt", "row", "col", None),
    )
    out_specs = P(("kpt", "row"), "col", None, None, None)
    return jax.shard_map(
        functools.partial(body, mesh.shape["kpt"], mesh.shape["row"], mesh.shape["col"]),
        mesh=mesh, in_specs=in_specs, out_specs=out_specs, check_vma=False,
    )
```

time: 163 us -> 151 us (0.926)
  Pallas kernels: 161 us -> 147 us
  local copies, waits for them, and re-layouts: 0.16 us -> 2.83 us
    pallas_call x2 -> x3, Pallas kernels: 161 us -> 147 us  [the longest x1 115 us: run(): pl.pallas_call(functools.partial(gather_kernel, n_row, n_col, options[at]...]
where the time goes in v1:
time: 151 us; the launch traced here: 152 us
  Pallas kernels  147 us (97%)
  local copies, waits for them, and re-layouts  2.83 us (2%)
    pallas_call x1, Pallas kernels, run(): pl.pallas_call(functools.partial(gather_kernel, n_row, n_col, options[at]...  115 us
    pallas_call x1, Pallas kernels, run(): pl.pallas_call(functools.partial(product_kernel, (n_row, n_col, sets, per...  18.4 us
    pallas_call x1, Pallas kernels, body(): pl.pallas_call(functools.partial(plan_kernel, (n_kpt, n_row, n_col, sets,...  13.8 us

profile of v1, /device:TPU:0, one launch (start us, length us, event | category | flops | bytes accessed | tf_op | source)
XLA Modules:
  0.0 151.8 jit_solution(4784197722510100898)
XLA Ops:
  0.0 0.7 compare_select_fusion
  0.7 0.7 fusion.1
  1.4 0.1 copy.19
  1.5 0.1 reshape.158
  1.6 0.1 broadcast_in_dim.19
  1.6 0.1 broadcast_in_dim.20
  1.7 0.1 copy.22
  1.8 0.1 reshape_reshape.3
  1.9 0.8 copy.20
  2.7 0.1 reshape.159
  2.8 0.8 copy.21
  3.6 0.1 reshape.160
  3.7 0.6 concatenate.3.tile
  4.3 13.8 %plan.1 = (s32[4,8,128]{2,1,0:T(8,128)S(1)}, s32[4,8,128]{2,1,0:T(8,128)S(1)}, s32[8,128]{1,0:T(8,128)S(1)}, s32[1]{0:T(128)}) custom-call(s32[8,128]{1,0:T(8,128)} %concatenate.3.tile), custom_call_target="tpu_custom_call" | custom-call | tf_op jit(solution)/shard_map/plan/pallas_call | solution.py:410
  18.7 133.1 %conditional.1 = (bf16[8,16,2,128,128]{4,3,2,1,0:T(8,128)(2,1)}) conditional(s32[]{:T(128)} %bitcast.20, (bf16[32,256,128]{2,1,0:T(8,128)(2,1)}, bf16[1,64,256,128]{3,2,1,0:T(8,128)(2,1)}, s32[8,128]{1,0:T(8,128)S(1)}, s32[4,8,128]{2,1,0:T(8,128)S(1)}, s32[4,8,128]{2,1,0:T(8,128)S(1)}) %tuple.49, ...), branch_computations={%region_1.2_spmd, %region_2.3_spmd, %region_3.4_spmd, %region_4.5_... | conditional | bytes 8 | solution.py:478
  18.7 114.7 %gather_panels_2.1 = (bf16[4,32,256,128]{3,2,1,0:T(8,128)(2,1)S(1)}, bf16[1,4,64,256,128]{4,3,2,1,0:T(8,128)(2,1)S(1)}) custom-call(bf16[32,256,128]{2,1,0:T(8,128)(2,1)} %get-tuple-element.87.left, bf16[1,64,256,128]{3,2,1,0:T(8,128)(2,1)} %get-tuple-element.88.right, s32[8,128]{1,0:T(8,128)S(1)} %get-tuple-element.89.table), custom_call_target="tpu_custom_call" | custom-call | tf_op jit(solution)/shard_map/cond/branch_2_fun/gather_panels_2/pallas_call | solution.py:433
  133.4 18.4 %pair_products.8 = bf16[128,256,128]{2,1,0:T(8,128)(2,1)} custom-call(bf16[128,256,128]{2,1,0:T(8,128)(2,1)S(1)} %bitcast.39, bf16[256,256,128]{2,1,0:T(8,128)(2,1)S(1)} %bitcast.33, s32[4,8,128]{2,1,0:T(8,128)S(1)} %get-tuple-element.92.left_meta, s32[4,8,128]{2,1,0:T(8,128)S(1)} %get-tuple-element.93.right_meta, s32[8,128]{1,0:T(8,128)S(1)} %get-tuple-element.89.table), custom_call_target="tpu_custom_call" | custom-call | tf_op jit(solution)/shard_map/cond/branch_2_fun/pair_products/pallas_call | solution.py:454
  (5 shorter events, 0.0 us)
